TPU v7x, 32 devices: a whole 2x2x4 slice. The times are simulated.
32 devices in a mesh: lat: 8 (over z, y), lon: 4 (over x, core).
Axes of the slice: x: 2, y: 2, z: 4, core: 2. Of those that a mesh axis runs over, the one named last changes fastest.
Arguments:
- x_fwd: bfloat16 [128, 384, 256], P('lat', 'lon'), may hold values from -6 to 6
- x_prev: bfloat16 [128, 384, 256], P('lat', 'lon'), may hold values from -6 to 6
- grad_out: bfloat16 [128, 384, 256], P('lat', 'lon'), may hold values from -6 to 6
- weight: bfloat16 [2048, 256], replicated, may hold values from -0.125 to 0.125
- basis: bfloat16 [128, 8, 3, 49], P('lat'), may hold values from -1.5 to 1.5
- lon_reach: int32 [128], P('lat'), may hold values from 1 to 24, as said below
- lat_reach: int32 [128], P('lat'), may hold values from 0 to 1, as said below
Outputs:
- output: bfloat16 [128, 384, 256], P('lat', 'lon')
- grad_in: bfloat16 [128, 384, 256], P('lat', 'lon')
- grad_weight: float32 [2048, 256], P(('lat', 'lon'))
Inputs may be any that keep to these rules, and one draw needn't show every extreme that they name: `lon_reach`: reaches widen toward the two poles; the cycles nearest the poles reach 24. `lat_reach`: the first and the last cycle of every aligned block of 16 cycles reach 1.
All inputs are finite; a program needn't handle non-finite values.
Results may differ from a plain program's by a relative error of at most 0.0049.
Values may be sent and summed in bfloat16 or wider, within the bound.
A program may use at most 192 MiB of HBM per device.

v0:
```python
import functools

import jax
import jax.numpy as jnp
from jax import lax
from jax.experimental import pallas as pl
from jax.experimental.pallas import tpu as pltpu
from jax.sharding import PartitionSpec as P


def shifted(value, axis, steps, periodic):
    count = lax.axis_size(axis)
    if periodic:
        pairs = [(source, (source + steps) % count) for source in range(count)]
    else:
        first, last = max(0, -steps), min(count, count - steps)
        pairs = [(source, source + steps) for source in range(first, last)]
    return lax.ppermute(value, axis, pairs)


def edges(block, low, high, reach):
    west = jnp.concatenate([low[None, :reach], block[:, :reach], high[None, :reach]], axis=0)
    east = jnp.concatenate([low[None, -reach:], block[:, -reach:], high[None, -reach:]], axis=0)
    from_west = shifted(east, "lon", 1, True)
    from_east = shifted(west, "lon", -1, True)
    return from_west, from_east


def tap_lanes(filters, span, lanes):
    rows, count, lat_taps, taps = filters.shape
    wide = jnp.pad(filters, ((0, 0), (0, 0), (0, 0), (0, span - taps)))
    wide = wide.reshape(rows, count, lat_taps * span)
    wide = jnp.pad(wide, ((0, 0), (0, 0), (0, lanes - lat_taps * span)))
    return wide.astype(jnp.float32)


def assemble(dest, own, low, high, west, east, reach):
    rows, cols, _ = own.shape
    span = cols + 2 * reach
    for row in range(rows + 2):
        start = row * span
        dest[start : start + reach, :] = west[row]
        dest[start + reach + cols : start + span, :] = east[row]
        if row == 0:
            dest[start + reach : start + reach + cols, :] = low[...]
        elif row == rows + 1:
            dest[start + reach : start + reach + cols, :] = high[...]
        else:
            dest[start + reach : start + reach + cols, :] = own[row - 1]
    tail = dest.shape[0] - (rows + 2) * span
    dest[(rows + 2) * span :, :] = jnp.zeros((tail, dest.shape[1]), dest.dtype)


def build(base, row, dest, cols):
    count, lanes = base.shape[1:]
    taps = base[row]
    for k in range(count):
        start = jnp.broadcast_to(taps[k : k + 1, :], (16, lanes))
        start = pltpu.roll(start, 0, 1, stride=1, stride_axis=0)
        for step in range(cols // 16):
            block = start if step == 0 else pltpu.roll(start, 16 * step, 1)
            dest[k * cols + step * 16 : k * cols + (step + 1) * 16, :] = block.astype(dest.dtype)


def convolve(toeplitz, field, row, span, conv, slot, cols, count):
    chans = field.shape[1]
    begin = pl.multiple_of(row * span, 16)
    window = field[pl.ds(begin, toeplitz.shape[1]), :]
    result = jnp.dot(toeplitz[...], window, preferred_element_type=jnp.float32)
    result = result.astype(jnp.bfloat16)
    place = pl.ds(pl.multiple_of(slot * cols, 16), cols)
    for k in range(count):
        conv[place, k * chans : (k + 1) * chans] = result[k * cols : (k + 1) * cols, :]


def weight_kernel(group, reach, base, own, low, high, west, east, grad, out, field, toeplitz, conv, total):
    step = pl.program_id(0)
    rows, cols, chans = own.shape
    count = base.shape[1]
    span = cols + 2 * reach

    @pl.when(step == 0)
    def _():
        assemble(field, own, low, high, west, east, reach)
        total[...] = jnp.zeros_like(total)

    def one(slot, carry):
        row = step * group + slot
        build(base, row, toeplitz, cols)
        convolve(toeplitz, field, row, span, conv, slot, cols, count)
        return carry

    lax.fori_loop(0, group, one, 0)
    cotangent = grad[...].reshape(group * cols, chans)
    total[...] += lax.dot_general(
        cotangent, conv[...], (((0,), (0,)), ((), ())), preferred_element_type=jnp.float32
    )

    @pl.when(step == pl.num_programs(0) - 1)
    def _():
        for k in range(count):
            out[k * chans : (k + 1) * chans, :] = total[:, k * chans : (k + 1) * chans].T.astype(out.dtype)


def field_kernel(group, reach, base, base_back, f_own, f_low, f_high, f_west, f_east, g_own, g_low, g_high, g_west, g_east, weight, weight_back, out, grad_in, f_field, g_field, toeplitz, toeplitz_back, f_conv, g_conv):
    step = pl.program_id(0)
    rows, cols, chans = f_own.shape
    count = base.shape[1]
    span = cols + 2 * reach

    @pl.when(step == 0)
    def _():
        assemble(f_field, f_own, f_low, f_high, f_west, f_east, reach)
        assemble(g_field, g_own, g_low, g_high, g_west, g_east, reach)

    def one(slot, carry):
        row = step * group + slot
        build(base, row, toeplitz, cols)
        build(base_back, row, toeplitz_back, cols)
        convolve(toeplitz, f_field, row, span, f_conv, slot, cols, count)
        convolve(toeplitz_back, g_field, row, span, g_conv, slot, cols, count)
        return carry

    lax.fori_loop(0, group, one, 0)
    mixed = jnp.dot(f_conv[...], weight[...], preferred_element_type=jnp.float32)
    out[...] = mixed.astype(out.dtype).reshape(out.shape)
    mixed = jnp.dot(g_conv[...], weight_back[...], preferred_element_type=jnp.float32)
    grad_in[...] = mixed.astype(grad_in.dtype).reshape(grad_in.shape)


def whole(array):
    rank = array.ndim
    return pl.BlockSpec(array.shape, lambda i: (0,) * rank)


def local(x_fwd, x_prev, grad_out, weight, basis, lon_reach, lat_reach):
    rows, cols, chans = x_fwd.shape
    _, count, lat_count, taps = basis.shape
    reach = (taps - 1) // 2
    span = cols + 2 * reach
    lanes = -(-lat_count * span // 256) * 256
    height = (rows - 1) * span + lanes
    height = max(height, (rows + 2) * span)
    group = 4 if rows % 4 == 0 else 1
    lat_taps = jnp.arange(lat_count, dtype=jnp.int32)
    lon_taps = jnp.arange(taps, dtype=jnp.int32)
    live = (jnp.abs(lat_taps - 1)[None, :, None] <= lat_reach[:, None, None]) & (
        jnp.abs(lon_taps - reach)[None, None, :] <= lon_reach[:, None, None]
    )
    filters = jnp.where(live[:, None, :, :], basis, jnp.zeros_like(basis))

    tiles = jnp.pad(
        filters[jnp.array([0, rows - 1])].reshape(2, count * lat_count, taps),
        ((0, 0), (0, 0), (0, chans - taps)),
    )
    prev_low = shifted(x_prev[-1], "lat", 1, False)
    prev_high = shifted(x_prev[0], "lat", -1, False)
    up = jnp.concatenate([x_fwd[-1], grad_out[-1], tiles[1]], axis=0)
    down = jnp.concatenate([x_fwd[0], grad_out[0], tiles[0]], axis=0)
    up = shifted(up, "lat", 1, False)
    down = shifted(down, "lat", -1, False)
    f_low, g_low, tile_low = up[:cols], up[cols : 2 * cols], up[2 * cols :, :taps]
    f_high, g_high, tile_high = down[:cols], down[cols : 2 * cols], down[2 * cols :, :taps]
    p_west, p_east = edges(x_prev, prev_low, prev_high, reach)
    f_west, f_east = edges(x_fwd, f_low, f_high, reach)
    g_west, g_east = edges(grad_out, g_low, g_high, reach)

    shape = (1, count, lat_count, taps)
    tall = jnp.concatenate([tile_low.reshape(shape), filters, tile_high.reshape(shape)], axis=0)
    flipped = tall[:, :, :, ::-1]
    back = jnp.stack(
        [flipped[a : a + rows, :, lat_count - 1 - a] for a in range(lat_count)], axis=2
    )
    base = tap_lanes(filters, span, lanes)
    base_back = tap_lanes(back, span, lanes)
    weight_back = weight.reshape(count, chans, chans).transpose(0, 2, 1).reshape(weight.shape)

    steps = rows // group
    limit = 60 * 1024 * 1024
    conv_flops = 2 * rows * count * cols * lanes * chans
    mix_flops = 2 * rows * cols * count * chans * chans
    blocked = pl.BlockSpec((group, cols, chans), lambda i: (i, 0, 0))
    operands = (base, x_prev, prev_low, prev_high, p_west, p_east)
    term = pl.pallas_call(
        functools.partial(weight_kernel, group, reach),
        grid=(steps,),
        in_specs=[whole(a) for a in operands] + [blocked],
        out_specs=pl.BlockSpec(weight.shape, lambda i: (0, 0)),
        out_shape=jax.ShapeDtypeStruct(weight.shape, jnp.bfloat16),
        scratch_shapes=[
            pltpu.VMEM((height, chans), jnp.bfloat16),
            pltpu.VMEM((count * cols, lanes), jnp.bfloat16),
            pltpu.VMEM((group * cols, count * chans), jnp.bfloat16),
            pltpu.VMEM((chans, count * chans), jnp.float32),
        ],
        compiler_params=pltpu.CompilerParams(vmem_limit_bytes=limit),
        cost_estimate=pl.CostEstimate(flops=conv_flops + mix_flops, bytes_accessed=4 << 20, transcendentals=0),
    )(*operands, grad_out)

    devices = lax.axis_size("lat") * lax.axis_size("lon")
    pieces = lax.all_to_all(
        term.reshape(devices, weight.shape[0] // devices, chans), ("lat", "lon"), 0, 0
    )

    operands = (base, base_back, x_fwd, f_low, f_high, f_west, f_east, grad_out, g_low, g_high, g_west, g_east, weight, weight_back)
    output, grad_in = pl.pallas_call(
        functools.partial(field_kernel, group, reach),
        grid=(steps,),
        in_specs=[whole(a) for a in operands],
        out_specs=[blocked, blocked],
        out_shape=[jax.ShapeDtypeStruct(x_fwd.shape, jnp.bfloat16)] * 2,
        scratch_shapes=[
            pltpu.VMEM((height, chans), jnp.bfloat16),
            pltpu.VMEM((height, chans), jnp.bfloat16),
            pltpu.VMEM((count * cols, lanes), jnp.bfloat16),
            pltpu.VMEM((count * cols, lanes), jnp.bfloat16),
            pltpu.VMEM((group * cols, count * chans), jnp.bfloat16),
            pltpu.VMEM((group * cols, count * chans), jnp.bfloat16),
        ],
        compiler_params=pltpu.CompilerParams(vmem_limit_bytes=limit),
        cost_estimate=pl.CostEstimate(flops=2 * (conv_flops + mix_flops), bytes_accessed=8 << 20, transcendentals=0),
    )(*operands)
    grad_weight = jnp.sum(pieces.astype(jnp.float32), axis=0)
    return output, grad_in, grad_weight


def solution(mesh):
    return jax.shard_map(
        local,
        mesh=mesh,
        in_specs=(
            P("lat", "lon", None),
            P("lat", "lon", None),
            P("lat", "lon", None),
            P(),
            P("lat", None, None, None),
            P("lat"),
            P("lat"),
        ),
        out_specs=(P("lat", "lon", None), P("lat", "lon", None), P(("lat", "lon"), None)),
        check_vma=False,
    )
```

profile of v0, /device:TPU:0, one launch (start us, length us, event | category | flops | bytes accessed | tf_op | source)
XLA Modules:
  0.0 106.0 jit_solution(3900504055718876059)
XLA Ops:
  0.7 0.8 broadcast_compare_fusion
  1.5 0.7 broadcast_compare_fusion.1
  2.3 1.0 broadcast_select_fusion
  3.9 0.8 slice_bitcast_fusion.5
  4.8 0.8 slice_bitcast_fusion.4
  6.2 5.5 %collective-permute-start = (bf16[216,256]{1,0:T(8,128)(2,1)}, bf16[216,256]{1,0:T(8,128)(2,1)}, u32[]{:S(2)}, u32[]{:S(2)}) collective-permute-start(bf16[216,256]{1,0:T(8,128)(2,1)} %pad_maximum_fusion.6), channel_id=1, source_target_pairs={{0,4},{4,8},{8,12},{12,16},{16,20},{20,24},{24,28},{1,5},{5,9},{9,... | collective-permute-start | bytes 331784 | tf_op jit(solution)/shard_map/ppermute | solution.py:18
  12.4 1.3 %collective-permute-start.1 = (bf16[216,256]{1,0:T(8,128)(2,1)}, bf16[216,256]{1,0:T(8,128)(2,1)}, u32[]{:S(2)}, u32[]{:S(2)}) collective-permute-start(bf16[216,256]{1,0:T(8,128)(2,1)} %pad_maximum_fusion.7), channel_id=1, source_target_pairs={{4,0},{8,4},{12,8},{16,12},{20,16},{24,20},{28,24},{5,1},{9,5},{13... | collective-permute-start | bytes 331784 | tf_op jit(solution)/shard_map/ppermute | solution.py:18
  14.4 5.2 %collective-permute-start.6 = (bf16[96,256]{1,0:T(8,128)(2,1)}, bf16[96,256]{1,0:T(8,128)(2,1)}, u32[]{:S(2)}, u32[]{:S(2)}) collective-permute-start(bf16[96,256]{1,0:T(8,128)(2,1)} %get-tuple-element.10), channel_id=1, source_target_pairs={{0,4},{4,8},{8,12},{12,16},{16,20},{20,24},{24,28},{1,5},{5,9},{9,... | collective-permute-start | bytes 147464 | tf_op jit(solution)/shard_map/ppermute | solution.py:18
  19.5 1.3 %collective-permute-start.7 = (bf16[96,256]{1,0:T(8,128)(2,1)S(1)}, bf16[96,256]{1,0:T(8,128)(2,1)}, u32[]{:S(2)}, u32[]{:S(2)}) collective-permute-start(bf16[96,256]{1,0:T(8,128)(2,1)S(1)} %get-tuple-element.9), channel_id=1, source_target_pairs={{4,0},{8,4},{12,8},{16,12},{20,16},{24,20},{28,24},{5,1},{9,5},{13... | collective-permute-start | bytes 147464 | tf_op jit(solution)/shard_map/ppermute | solution.py:18
  20.8 1.1 fusion.4
  22.3 0.7 pad_convert_fusion.1.base
  23.1 1.3 %copy.23 = bf16[8,256,256]{1,2,0:T(8,128)(2,1)} copy(bf16[8,256,256]{2,1,0:T(8,128)(2,1)S(1)} %bitcast.46) | data formatting | bytes 2097152 | tf_op jit(solution)/shard_map/reshape | solution.py:176
  24.4 0.7 slice_bitcast_fusion.7
  25.6 0.7 slice_bitcast_fusion.6
  26.5 1.8 %collective-permute-start.9 = (bf16[18,24,256]{2,1,0:T(8,128)(2,1)S(1)}, bf16[18,24,256]{2,1,0:T(8,128)(2,1)S(1)}, u32[]{:S(2)}, u32[]{:S(2)}) collective-permute-start(bf16[18,24,256]{2,1,0:T(8,128)(2,1)S(1)} %pad_maximum_fusion.5), channel_id=1, source_target_pairs={{0,3},{1,0},{2,1},{3,2},{4,7},{5,4},{6,5},{7,6},{8,11},{9,8},{10,9... | collective-permute-start | bytes 663560 | tf_op jit(solution)/shard_map/ppermute | solution.py:18
  28.2 0.7 slice.165
  29.0 0.7 slice.167
  30.0 0.8 slice_bitcast_fusion.11
  30.8 0.8 slice_bitcast_fusion.10
  31.5 0.7 collective-permute-done.8.west
  32.3 0.9 collective-permute-done.9.east
  33.8 16.1 %shard_map.104 = bf16[2048,256]{1,0:T(8,128)(2,1)} custom-call(f32[16,8,512]{2,1,0:T(8,128)} %pad_convert_fusion.1.base, bf16[16,96,256]{2,1,0:T(8,128)(2,1)} %own.1, bf16[96,256]{1,0:T(8,128)(2,1)} %collective-permute-done.6.low, bf16[96,256]{1,0:T(8,128)(2,1)} %collective-permute-done.7.high, bf16[18,24,256]{2,1,0:T(8,128)(2,1)} %copy-done.3, ...), custom_call_target="tpu_custom_call" | custom-call | flops 4831838208 | bytes 4194304 | tf_op jit(solution)/shard_map/pallas_call | solution.py:184
  49.9 7.3 %all-to-all-start = ((bf16[32,64,256]{2,1,0:T(8,128)(2,1)}), bf16[32,64,256]{2,1,0:T(8,128)(2,1)S(1)}, u32[]{:S(2)}, u32[]{:S(2)}) async-start(bf16[32,64,256]{2,1,0:T(8,128)(2,1)} %bitcast.48), calls=%async_computation | async-start | bytes 2097152 | tf_op jit(solution)/shard_map/all_to_all | solution.py:201
  58.0 1.5 %collective-permute-start.3 = (bf16[18,24,256]{2,1,0:T(8,128)(2,1)S(1)}, bf16[18,24,256]{2,1,0:T(8,128)(2,1)S(1)}, u32[]{:S(2)}, u32[]{:S(2)}) collective-permute-start(bf16[18,24,256]{2,1,0:T(8,128)(2,1)S(1)} %pad_maximum_fusion.1), channel_id=1, source_target_pairs={{0,3},{1,0},{2,1},{3,2},{4,7},{5,4},{6,5},{7,6},{8,11},{9,8},{10,9... | collective-permute-start | bytes 663560 | tf_op jit(solution)/shard_map/ppermute | solution.py:18
  59.8 1.6 %collective-permute-start.5 = (bf16[18,24,256]{2,1,0:T(8,128)(2,1)S(1)}, bf16[18,24,256]{2,1,0:T(8,128)(2,1)S(1)}, u32[]{:S(2)}, u32[]{:S(2)}) collective-permute-start(bf16[18,24,256]{2,1,0:T(8,128)(2,1)S(1)} %pad_maximum_fusion.3), channel_id=1, source_target_pairs={{0,3},{1,0},{2,1},{3,2},{4,7},{5,4},{6,5},{7,6},{8,11},{9,8},{10,9... | collective-permute-start | bytes 663560 | tf_op jit(solution)/shard_map/ppermute | solution.py:18
  61.4 0.8 pad_convert_fusion.base_back
  62.2 1.5 %fusion.5 = (bf16[96,256]{1,0:T(8,128)(2,1)}, bf16[96,256]{1,0:T(8,128)(2,1)}) fusion(bf16[216,256]{1,0:T(8,128)(2,1)} %collective-permute-done.1), kind=kLoop, calls=%fused_computation.48 | loop fusion | bytes 196608 | tf_op jit(solution)/shard_map/slice | solution.py:163
  63.7 1.5 %fusion.6 = (bf16[96,256]{1,0:T(8,128)(2,1)}, bf16[96,256]{1,0:T(8,128)(2,1)}) fusion(bf16[216,256]{1,0:T(8,128)(2,1)} %collective-permute-done), kind=kLoop, calls=%fused_computation.49 | loop fusion | bytes 196608 | tf_op jit(solution)/shard_map/slice | solution.py:162
  65.1 8.0 %collective-permute-done.2.f_west = bf16[18,24,256]{2,1,0:T(8,128)(2,1)S(1)} collective-permute-done((bf16[18,24,256]{2,1,0:T(8,128)(2,1)S(1)}, bf16[18,24,256]{2,1,0:T(8,128)(2,1)S(1)}, u32[]{:S(2)}, u32[]{:S(2)}) %collective-permute-start.2) | collective-permute-done | bytes 221216 | tf_op jit(solution)/shard_map/ppermute | solution.py:18
  73.2 5.6 %collective-permute-done.4.g_west = bf16[18,24,256]{2,1,0:T(8,128)(2,1)S(1)} collective-permute-done((bf16[18,24,256]{2,1,0:T(8,128)(2,1)S(1)}, bf16[18,24,256]{2,1,0:T(8,128)(2,1)S(1)}, u32[]{:S(2)}, u32[]{:S(2)}) %collective-permute-start.4) | collective-permute-done | bytes 221216 | tf_op jit(solution)/shard_map/ppermute | solution.py:18
  79.6 25.7 %shard_map.103 = (bf16[16,96,256]{2,1,0:T(8,128)(2,1)}, bf16[16,96,256]{2,1,0:T(8,128)(2,1)}) custom-call(f32[16,8,512]{2,1,0:T(8,128)} %pad_convert_fusion.1.base, f32[16,8,512]{2,1,0:T(8,128)} %pad_convert_fusion.base_back, bf16[16,96,256]{2,1,0:T(8,128)(2,1)} %f_own.1, bf16[96,256]{1,0:T(8,128)(2,1)} %get-tuple-element.30.f_low, ...), custom_call_target="tpu_custom_call" | custom-call | flops 9663676416 | bytes 8388608 | tf_op jit(solution)/shard_map/pallas_call | solution.py:206
  105.2 0.8 convert_reduce_fusion
  (63 shorter events, 6.4 us)
Async XLA Ops:
  0.6 13.1 %copy-start.1 = (bf16[16,96,256]{2,1,0:T(8,128)(2,1)S(1)}, bf16[16,96,256]{2,1,0:T(8,128)(2,1)}, u32[]{:S(2)}) copy-start(bf16[16,96,256]{2,1,0:T(8,128)(2,1)} %own.1) | copy-start | bytes 2359300
  2.3 19.6 %copy-start.2 = (bf16[16,96,256]{2,1,0:T(8,128)(2,1)S(1)}, bf16[16,96,256]{2,1,0:T(8,128)(2,1)}, u32[]{:S(2)}) copy-start(bf16[16,96,256]{2,1,0:T(8,128)(2,1)} %grad.1) | copy-start | bytes 2359300
  6.2 22.0 %collective-permute-start = (bf16[216,256]{1,0:T(8,128)(2,1)}, bf16[216,256]{1,0:T(8,128)(2,1)}, u32[]{:S(2)}, u32[]{:S(2)}) collective-permute-start(bf16[216,256]{1,0:T(8,128)(2,1)} %pad_maximum_fusion.6), channel_id=1, source_target_pairs={{0,4},{4,8},{8,12},{12,16},{16,20},{20,24},{24,28},{1,5},{5,9},{9,... | collective-permute-start | bytes 331784 | tf_op jit(solution)/shard_map/ppermute | solution.py:18
  12.4 16.5 %collective-permute-start.1 = (bf16[216,256]{1,0:T(8,128)(2,1)}, bf16[216,256]{1,0:T(8,128)(2,1)}, u32[]{:S(2)}, u32[]{:S(2)}) collective-permute-start(bf16[216,256]{1,0:T(8,128)(2,1)} %pad_maximum_fusion.7), channel_id=1, source_target_pairs={{4,0},{8,4},{12,8},{16,12},{20,16},{24,20},{28,24},{5,1},{9,5},{13... | collective-permute-start | bytes 331784 | tf_op jit(solution)/shard_map/ppermute | solution.py:18
  14.4 10.1 %collective-permute-start.6 = (bf16[96,256]{1,0:T(8,128)(2,1)}, bf16[96,256]{1,0:T(8,128)(2,1)}, u32[]{:S(2)}, u32[]{:S(2)}) collective-permute-start(bf16[96,256]{1,0:T(8,128)(2,1)} %get-tuple-element.10), channel_id=1, source_target_pairs={{0,4},{4,8},{8,12},{12,16},{16,20},{20,24},{24,28},{1,5},{5,9},{9,... | collective-permute-start | bytes 147464 | tf_op jit(solution)/shard_map/ppermute | solution.py:18
  19.5 6.1 %collective-permute-start.7 = (bf16[96,256]{1,0:T(8,128)(2,1)S(1)}, bf16[96,256]{1,0:T(8,128)(2,1)}, u32[]{:S(2)}, u32[]{:S(2)}) collective-permute-start(bf16[96,256]{1,0:T(8,128)(2,1)S(1)} %get-tuple-element.9), channel_id=1, source_target_pairs={{4,0},{8,4},{12,8},{16,12},{20,16},{24,20},{28,24},{5,1},{9,5},{13... | collective-permute-start | bytes 147464 | tf_op jit(solution)/shard_map/ppermute | solution.py:18
  21.9 1.2 %copy-start = (bf16[2048,256]{1,0:T(8,128)(2,1)S(1)}, bf16[2048,256]{1,0:T(8,128)(2,1)}, u32[]{:S(2)}) copy-start(bf16[2048,256]{1,0:T(8,128)(2,1)} %weight.1) | copy-start | bytes 3145732
  26.4 5.9 %collective-permute-start.8 = (bf16[18,24,256]{2,1,0:T(8,128)(2,1)S(1)}, bf16[18,24,256]{2,1,0:T(8,128)(2,1)S(1)}, u32[]{:S(2)}, u32[]{:S(2)}) collective-permute-start(bf16[18,24,256]{2,1,0:T(8,128)(2,1)S(1)} %pad_maximum_fusion.4), channel_id=1, source_target_pairs={{0,1},{1,2},{2,3},{3,0},{4,5},{5,6},{6,7},{7,4},{8,9},{9,10},{10,1... | collective-permute-start | bytes 663560 | tf_op jit(solution)/shard_map/ppermute | solution.py:18
  26.5 6.7 %collective-permute-start.9 = (bf16[18,24,256]{2,1,0:T(8,128)(2,1)S(1)}, bf16[18,24,256]{2,1,0:T(8,128)(2,1)S(1)}, u32[]{:S(2)}, u32[]{:S(2)}) collective-permute-start(bf16[18,24,256]{2,1,0:T(8,128)(2,1)S(1)} %pad_maximum_fusion.5), channel_id=1, source_target_pairs={{0,3},{1,0},{2,1},{3,2},{4,7},{5,4},{6,5},{7,6},{8,11},{9,8},{10,9... | collective-permute-start | bytes 663560 | tf_op jit(solution)/shard_map/ppermute | solution.py:18
  32.3 0.9 copy-start.3
  33.1 0.7 copy-start.5
  49.9 55.3 %all-to-all-start = ((bf16[32,64,256]{2,1,0:T(8,128)(2,1)}), bf16[32,64,256]{2,1,0:T(8,128)(2,1)S(1)}, u32[]{:S(2)}, u32[]{:S(2)}) async-start(bf16[32,64,256]{2,1,0:T(8,128)(2,1)} %bitcast.48), calls=%async_computation | async-start | bytes 2097152 | tf_op jit(solution)/shard_map/all_to_all | solution.py:201
  57.6 15.5 %collective-permute-start.2 = (bf16[18,24,256]{2,1,0:T(8,128)(2,1)S(1)}, bf16[18,24,256]{2,1,0:T(8,128)(2,1)S(1)}, u32[]{:S(2)}, u32[]{:S(2)}) collective-permute-start(bf16[18,24,256]{2,1,0:T(8,128)(2,1)S(1)} %pad_maximum_fusion), channel_id=1, source_target_pairs={{0,1},{1,2},{2,3},{3,0},{4,5},{5,6},{6,7},{7,4},{8,9},{9,10},{10,1... | collective-permute-start | bytes 663560 | tf_op jit(solution)/shard_map/ppermute | solution.py:18
  58.0 15.2 %collective-permute-start.3 = (bf16[18,24,256]{2,1,0:T(8,128)(2,1)S(1)}, bf16[18,24,256]{2,1,0:T(8,128)(2,1)S(1)}, u32[]{:S(2)}, u32[]{:S(2)}) collective-permute-start(bf16[18,24,256]{2,1,0:T(8,128)(2,1)S(1)} %pad_maximum_fusion.1), channel_id=1, source_target_pairs={{0,3},{1,0},{2,1},{3,2},{4,7},{5,4},{6,5},{7,6},{8,11},{9,8},{10,9... | collective-permute-start | bytes 663560 | tf_op jit(solution)/shard_map/ppermute | solution.py:18
  59.6 19.2 %collective-permute-start.4 = (bf16[18,24,256]{2,1,0:T(8,128)(2,1)S(1)}, bf16[18,24,256]{2,1,0:T(8,128)(2,1)S(1)}, u32[]{:S(2)}, u32[]{:S(2)}) collective-permute-start(bf16[18,24,256]{2,1,0:T(8,128)(2,1)S(1)} %pad_maximum_fusion.2), channel_id=1, source_target_pairs={{0,1},{1,2},{2,3},{3,0},{4,5},{5,6},{6,7},{7,4},{8,9},{9,10},{10,1... | collective-permute-start | bytes 663560 | tf_op jit(solution)/shard_map/ppermute | solution.py:18
  59.8 19.0 %collective-permute-start.5 = (bf16[18,24,256]{2,1,0:T(8,128)(2,1)S(1)}, bf16[18,24,256]{2,1,0:T(8,128)(2,1)S(1)}, u32[]{:S(2)}, u32[]{:S(2)}) collective-permute-start(bf16[18,24,256]{2,1,0:T(8,128)(2,1)S(1)} %pad_maximum_fusion.3), channel_id=1, source_target_pairs={{0,3},{1,0},{2,1},{3,2},{4,7},{5,4},{6,5},{7,6},{8,11},{9,8},{10,9... | collective-permute-start | bytes 663560 | tf_op jit(solution)/shard_map/ppermute | solution.py:18
  73.2 5.6 %copy-start.4 = (bf16[18,24,256]{2,1,0:T(8,128)(2,1)}, bf16[18,24,256]{2,1,0:T(8,128)(2,1)S(1)}, u32[]{:S(2)}) copy-start(bf16[18,24,256]{2,1,0:T(8,128)(2,1)S(1)} %collective-permute-done.2.f_west) | copy-start | bytes 663556
  73.2 5.6 %copy-start.6 = (bf16[18,24,256]{2,1,0:T(8,128)(2,1)}, bf16[18,24,256]{2,1,0:T(8,128)(2,1)S(1)}, u32[]{:S(2)}) copy-start(bf16[18,24,256]{2,1,0:T(8,128)(2,1)S(1)} %collective-permute-done.3.f_east) | copy-start | bytes 663556
  78.8 0.7 copy-start.7
  78.8 0.8 copy-start.8
where the time goes:
time: 107 us; the launch traced here: 106 us
  Pallas kernels  41.8 us (39%)
  starting transfers between devices  26.1 us (24%)
  waiting for transfers between devices  15.7 us (15%)
  local copies, waits for them, and re-layouts  15.1 us (14%)
  other arithmetic  6.44 us (6%)
    pallas_call x1, Pallas kernels, local(): pl.pallas_call(functools.partial(field_kernel, group, reach), grid=(steps...  25.7 us
    ppermute x10, starting transfers between devices, shifted(): return lax.ppermute(value, axis, pairs)  18.8 us
    pallas_call x1, Pallas kernels, local(): pl.pallas_call(functools.partial(weight_kernel, group, reach), grid=(step...  16.1 us
    ppermute x10, waiting for transfers between devices, shifted(): return lax.ppermute(value, axis, pairs)  15.7 us
    all_to_all x1, starting transfers between devices, local(): lax.all_to_all(term.reshape(devices, weight.shape[0] // devices, chans),...  7.3 us
  transfers between devices with their start and end apart: 11, of which 5 were waited for; matrix products, arithmetic and copies ran while one was open for 13% of the time, Pallas kernels for 24%

commit v1 on v0

v1 whole, which is shorter than its diff:
```python
import functools

import jax
import jax.numpy as jnp
from jax import lax
from jax.experimental import pallas as pl
from jax.experimental.pallas import tpu as pltpu
from jax.sharding import PartitionSpec as P


MESH = pl.DeviceIdType.MESH


def tap_lanes(taps, span, lanes):
    rows, count, lat_taps, width = taps.shape
    wide = jnp.pad(taps, ((0, 0), (0, 0), (0, 0), (0, span - width)))
    wide = wide.reshape(rows, count, lat_taps * span)
    return jnp.pad(wide, ((0, 0), (0, 0), (0, lanes - lat_taps * span)))


def halo_copies(own, low, high, west, east, reach, send, recv, first):
    rows, cols, _ = own.shape
    lat, lon = lax.axis_index("lat"), lax.axis_index("lon")
    lats, lons = lax.axis_size("lat"), lax.axis_size("lon")
    up, down = lax.rem(lat + 1, lats), lax.rem(lat + lats - 1, lats)
    right, left = lax.rem(lon + 1, lons), lax.rem(lon + lons - 1, lons)
    east_edge, west_edge = pl.ds(cols - reach, reach), pl.ds(0, reach)
    moves = (
        (own.at[:, east_edge], west.at[pl.ds(1, rows)], lat, right),
        (own.at[:, west_edge], east.at[pl.ds(1, rows)], lat, left),
        (own.at[rows - 1], low, up, lon),
        (own.at[0], high, down, lon),
        (own.at[rows - 1, east_edge], west.at[0], up, right),
        (own.at[rows - 1, west_edge], east.at[0], up, left),
        (own.at[0, east_edge], west.at[rows + 1], down, right),
        (own.at[0, west_edge], east.at[rows + 1], down, left),
    )
    return [
        pltpu.make_async_remote_copy(
            src_ref=source,
            dst_ref=target,
            send_sem=send.at[first + n],
            recv_sem=recv.at[first + n],
            device_id={"lat": lat_id, "lon": lon_id},
            device_id_type=MESH,
        )
        for n, (source, target, lat_id, lon_id) in enumerate(moves)
    ]


def assemble(dest, own, low, high, west, east, reach):
    rows, cols, _ = own.shape
    span = cols + 2 * reach
    for row in range(rows + 2):
        start = row * span
        dest[start : start + reach, :] = west[row]
        dest[start + reach + cols : start + span, :] = east[row]
        if row == 0:
            dest[start + reach : start + reach + cols, :] = low[...]
        elif row == rows + 1:
            dest[start + reach : start + reach + cols, :] = high[...]
        else:
            dest[start + reach : start + reach + cols, :] = own[row - 1]
    tail = dest.shape[0] - (rows + 2) * span
    dest[(rows + 2) * span :, :] = jnp.zeros((tail, dest.shape[1]), dest.dtype)


def build(taps, dest, cols):
    count, lanes = taps.shape
    for k in range(count):
        start = jnp.broadcast_to(taps[k : k + 1, :], (16, lanes))
        start = pltpu.roll(start, 0, 1, stride=1, stride_axis=0)
        for step in range(cols // 16):
            block = start if step == 0 else pltpu.roll(start, 16 * step, 1)
            dest[k * cols + step * 16 : k * cols + (step + 1) * 16, :] = block.astype(dest.dtype)


def convolve(toeplitz, field, row, span, conv, slot, cols, count):
    chans = field.shape[1]
    begin = pl.multiple_of(row * span, 16)
    window = field[pl.ds(begin, toeplitz.shape[1]), :]
    result = jnp.dot(toeplitz[...], window, preferred_element_type=jnp.float32)
    result = result.astype(jnp.bfloat16)
    place = pl.ds(pl.multiple_of(slot * cols, 16), cols)
    for k in range(count):
        conv[place, k * chans : (k + 1) * chans] = result[k * cols : (k + 1) * cols, :]


def weight_kernel(group, reach, base, back, own, f_own, g_own, g_hbm, term, f_low, f_high, f_west, f_east, g_low, g_high, g_west, g_east, b_low, b_high, low, high, west, east, q_low, q_high, field, even, odd, conv, total, send, recv):
    rows, cols, chans = own.shape
    count = base.shape[1]
    span = cols + 2 * reach
    lat, lon = lax.axis_index("lat"), lax.axis_index("lon")
    lats, lons = lax.axis_size("lat"), lax.axis_size("lon")
    barrier = pltpu.get_barrier_semaphore()
    for lat_move in (1, 0, lats - 1):
        for lon_move in (1, 0, lons - 1):
            if lat_move or lon_move:
                pl.semaphore_signal(
                    barrier,
                    inc=1,
                    device_id={"lat": lax.rem(lat + lat_move, lats), "lon": lax.rem(lon + lon_move, lons)},
                    device_id_type=MESH,
                )
    pl.semaphore_wait(barrier, 8)
    now = halo_copies(own, low, high, west, east, reach, send, recv, 0)
    later = halo_copies(f_own, f_low, f_high, f_west, f_east, reach, send, recv, 8)
    later += halo_copies(g_hbm, g_low, g_high, g_west, g_east, reach, send, recv, 16)
    for n, (source, target, move) in enumerate(((rows - 1, q_low, 1), (0, q_high, lats - 1))):
        later.append(
            pltpu.make_async_remote_copy(
                src_ref=back.at[source],
                dst_ref=target,
                send_sem=send.at[24 + n],
                recv_sem=recv.at[24 + n],
                device_id={"lat": lax.rem(lat + move, lats), "lon": lon},
                device_id_type=MESH,
            )
        )
    for copy in now + later:
        copy.start()
    build(base[0], even, cols)
    total[...] = jnp.zeros_like(total)
    for copy in now:
        copy.wait()
    assemble(field, own, low, high, west, east, reach)

    def pair(number, carry):
        row = number * 2
        slot = lax.rem(row, group)
        build(base[row + 1], odd, cols)
        convolve(even, field, row, span, conv, slot, cols, count)
        build(base[lax.rem(row + 2, rows)], even, cols)
        convolve(odd, field, row + 1, span, conv, slot + 1, cols, count)
        return carry

    def several(step, carry):
        lax.fori_loop(step * (group // 2), (step + 1) * (group // 2), pair, 0)
        cotangent = g_own[pl.ds(step * group, group)].reshape(group * cols, chans)
        total[...] += lax.dot_general(
            cotangent, conv[...], (((0,), (0,)), ((), ())), preferred_element_type=jnp.float32
        )
        return carry

    lax.fori_loop(0, rows // group, several, 0)
    for k in range(count):
        term[k * chans : (k + 1) * chans, :] = total[:, k * chans : (k + 1) * chans].T.astype(term.dtype)
    for copy in later:
        copy.wait()
    b_low[...] = jnp.where(lat == 0, jnp.zeros_like(b_low), q_low[...])
    b_high[...] = jnp.where(lat == lats - 1, jnp.zeros_like(b_high), q_high[...])


def field_kernel(group, reach, base, back, b_low, b_high, f_own, f_low, f_high, f_west, f_east, g_own, g_low, g_high, g_west, g_east, weight, weight_back, out, grad_in, f_field, g_field, taps, f_even, f_odd, g_even, g_odd, f_conv, g_conv):
    step = pl.program_id(0)
    rows, cols, chans = f_own.shape
    count, lanes = base.shape[1:]
    span = cols + 2 * reach
    lane = lax.broadcasted_iota(jnp.int32, (count, lanes), 1)

    def back_taps(row):
        return jnp.where(lane < span, taps[row], jnp.where(lane < 2 * span, taps[row + 1], taps[row + 2]))

    @pl.when(step == 0)
    def _():
        assemble(f_field, f_own, f_low, f_high, f_west, f_east, reach)
        assemble(g_field, g_own, g_low, g_high, g_west, g_east, reach)
        taps[0] = b_low[...]
        taps[pl.ds(1, rows)] = back[...]
        taps[rows + 1] = b_high[...]
        build(base[0], f_even, cols)
        build(back_taps(0), g_even, cols)

    def pair(number, carry):
        slot = number * 2
        row = step * group + slot
        follow = lax.rem(row + 2, rows)
        build(base[row + 1], f_odd, cols)
        convolve(f_even, f_field, row, span, f_conv, slot, cols, count)
        build(back_taps(row + 1), g_odd, cols)
        convolve(g_even, g_field, row, span, g_conv, slot, cols, count)
        build(base[follow], f_even, cols)
        convolve(f_odd, f_field, row + 1, span, f_conv, slot + 1, cols, count)
        build(back_taps(follow), g_even, cols)
        convolve(g_odd, g_field, row + 1, span, g_conv, slot + 1, cols, count)
        return carry

    lax.fori_loop(0, group // 2, pair, 0)
    mixed = jnp.dot(f_conv[...], weight[...], preferred_element_type=jnp.float32)
    out[...] = mixed.astype(out.dtype).reshape(out.shape)
    mixed = jnp.dot(g_conv[...], weight_back[...], preferred_element_type=jnp.float32)
    grad_in[...] = mixed.astype(grad_in.dtype).reshape(grad_in.shape)


def whole(array):
    rank = array.ndim
    return pl.BlockSpec(array.shape, lambda i: (0,) * rank)


def local(x_fwd, x_prev, grad_out, weight, basis, lon_reach, lat_reach):
    rows, cols, chans = x_fwd.shape
    _, count, lat_count, taps = basis.shape
    reach = (taps - 1) // 2
    span = cols + 2 * reach
    lanes = -(-lat_count * span // 256) * 256
    height = (rows - 1) * span + lanes
    height = max(height, (rows + 2) * span)
    group = 4 if rows % 4 == 0 else 2
    lats = lax.axis_size("lat")
    place = jnp.arange(lanes, dtype=jnp.int32)
    lat_tap, lon_tap = place // span, place % span
    row_ids = lax.axis_index("lat") * rows + jnp.arange(rows, dtype=jnp.int32)
    live = (jnp.abs(lat_tap - 1)[None, :] <= lat_reach[:, None]) & (
        jnp.abs(lon_tap - reach)[None, :] <= lon_reach[:, None]
    )
    source = row_ids[:, None] + lat_tap[None, :] - 1
    inside = live & (source >= 0) & (source < rows * lats)
    base = tap_lanes(basis, span, lanes)
    base = jnp.where(inside[:, None, :], base, jnp.zeros_like(base)).astype(jnp.float32)
    back = tap_lanes(basis[:, :, ::-1, ::-1], span, lanes)
    back = jnp.where(live[:, None, :], back, jnp.zeros_like(back)).astype(jnp.float32)
    weight_back = weight.reshape(count, chans, chans).transpose(0, 2, 1).reshape(weight.shape)

    steps = rows // group
    limit = 60 * 1024 * 1024
    conv_flops = 2 * rows * count * cols * lanes * chans
    mix_flops = 2 * rows * cols * count * chans * chans
    blocked = pl.BlockSpec((group, cols, chans), lambda i: (i, 0, 0))
    vmem, anywhere = pl.BlockSpec(memory_space=pltpu.VMEM), pl.BlockSpec(memory_space=pl.ANY)
    line = jax.ShapeDtypeStruct((cols, chans), jnp.bfloat16)
    side = jax.ShapeDtypeStruct((rows + 2, reach, chans), jnp.bfloat16)
    tile = jax.ShapeDtypeStruct((count, lanes), jnp.float32)
    band = pltpu.VMEM((height, chans), jnp.bfloat16)
    square = pltpu.VMEM((count * cols, lanes), jnp.bfloat16)
    wide = pltpu.VMEM((group * cols, count * chans), jnp.bfloat16)
    term, f_low, f_high, f_west, f_east, g_low, g_high, g_west, g_east, b_low, b_high = pl.pallas_call(
        functools.partial(weight_kernel, group, reach),
        in_specs=[vmem, anywhere, vmem, anywhere, vmem, anywhere],
        out_specs=[vmem] + [anywhere] * 8 + [vmem] * 2,
        out_shape=[jax.ShapeDtypeStruct(weight.shape, jnp.bfloat16)] + [line, line, side, side] * 2 + [tile] * 2,
        scratch_shapes=[
            pltpu.VMEM(line.shape, line.dtype),
            pltpu.VMEM(line.shape, line.dtype),
            pltpu.VMEM(side.shape, side.dtype),
            pltpu.VMEM(side.shape, side.dtype),
            pltpu.VMEM(tile.shape, tile.dtype),
            pltpu.VMEM(tile.shape, tile.dtype),
            band,
            square,
            square,
            wide,
            pltpu.VMEM((chans, count * chans), jnp.float32),
            pltpu.SemaphoreType.DMA((26,)),
            pltpu.SemaphoreType.DMA((26,)),
        ],
        compiler_params=pltpu.CompilerParams(vmem_limit_bytes=limit, collective_id=0, has_side_effects=True),
        cost_estimate=pl.CostEstimate(flops=conv_flops + mix_flops, bytes_accessed=4 << 20, transcendentals=0),
    )(base, back, x_prev, x_fwd, grad_out, grad_out)

    devices = lax.axis_size("lat") * lax.axis_size("lon")
    pieces = lax.all_to_all(
        term.reshape(devices, weight.shape[0] // devices, chans), ("lat", "lon"), 0, 0
    )

    operands = (base, back, b_low, b_high, x_fwd, f_low, f_high, f_west, f_east, grad_out, g_low, g_high, g_west, g_east, weight, weight_back)
    output, grad_in = pl.pallas_call(
        functools.partial(field_kernel, group, reach),
        grid=(steps,),
        in_specs=[whole(a) for a in operands],
        out_specs=[blocked, blocked],
        out_shape=[jax.ShapeDtypeStruct(x_fwd.shape, jnp.bfloat16)] * 2,
        scratch_shapes=[band, band, pltpu.VMEM((rows + 2, count, lanes), jnp.float32)]
        + [square] * 4
        + [wide] * 2,
        compiler_params=pltpu.CompilerParams(vmem_limit_bytes=limit),
        cost_estimate=pl.CostEstimate(flops=2 * (conv_flops + mix_flops), bytes_accessed=8 << 20, transcendentals=0),
    )(*operands)
    grad_weight = jnp.sum(pieces.astype(jnp.float32), axis=0)
    return output, grad_in, grad_weight


def solution(mesh):
    return jax.shard_map(
        local,
        mesh=mesh,
        in_specs=(
            P("lat", "lon", None),
            P("lat", "lon", None),
            P("lat", "lon", None),
            P(),
            P("lat", None, None, None),
            P("lat"),
            P("lat"),
        ),
        out_specs=(P("lat", "lon", None), P("lat", "lon", None), P(("lat", "lon"), None)),
        check_vma=False,
    )
```

time: 107 us -> 73.6 us (0.69)
  starting transfers between devices: 26.1 us -> 3.5 us
  Pallas kernels: 41.8 us -> 63.3 us
  waiting for transfers between devices: 15.7 us -> 0.01 us
  local copies, waits for them, and re-layouts: 15.1 us -> 3.88 us
  other arithmetic: 6.44 us -> 1.8 us
    ppermute x10 -> x0, starting transfers between devices: 18.8 us -> none  [shifted(): return lax.ppermute(value, axis, pairs)]
    ppermute x10 -> x0, waiting for transfers between devices: 15.7 us -> none  [shifted(): return lax.ppermute(value, axis, pairs)]
    pallas_call x1, Pallas kernels: 16.1 us -> 30.8 us  [local(): pl.pallas_call(functools.partial(weight_kernel, group, reach), in_specs=[...]
    pallas_call x1, Pallas kernels: 25.7 us -> 32.5 us  [local(): pl.pallas_call(functools.partial(field_kernel, group, reach), grid=(steps...]
    slice x10 -> x0, local copies, waits for them, and re-layouts: 5.72 us -> none  [the longest x1 1.48 us: local(): up[cols:2 * cols]]
    all_to_all x1, starting transfers between devices: 7.3 us -> 3.5 us  [local(): lax.all_to_all(term.reshape(devices, weight.shape[0] // devices, chans),...]
    broadcast_in_dim x4 -> x0, local copies, waits for them, and re-layouts: 2.98 us -> none  [the longest x2 1.49 us: edges(): low[None, :reach]]
    squeeze x4 -> x0, local copies, waits for them, and re-layouts: 2.3 us -> none  [the longest x3 1.67 us: local(): up = jnp.concatenate([x_fwd[-1], grad_out[-1], tiles[1]], axis=0)]
  transfers between devices with their start and end apart: 11 -> 1, of which waited for: 5 -> 0; matrix products, arithmetic and copies ran while one was open for 13% -> 2% of each run, Pallas kernels for 24% -> 44%
where the time goes in v1:
time: 73.6 us; the launch traced here: 73.3 us
  Pallas kernels  63.3 us (86%)
  local copies, waits for them, and re-layouts  3.88 us (5%)
  starting transfers between devices  3.5 us (5%)
  other arithmetic  1.8 us (2%)
  between operations  0.78 us (1%)
    pallas_call x1, Pallas kernels, local(): pl.pallas_call(functools.partial(field_kernel, group, reach), grid=(steps...  32.5 us
    pallas_call x1, Pallas kernels, local(): pl.pallas_call(functools.partial(weight_kernel, group, reach), in_specs=[...  30.8 us
    all_to_all x1, starting transfers between devices, local(): lax.all_to_all(term.reshape(devices, weight.shape[0] // devices, chans),...  3.5 us
  transfers between devices with their start and end apart: 1, of which 0 were waited for; matrix products, arithmetic and copies ran while one was open for 2% of the time, Pallas kernels for 44%

profile of v1, /device:TPU:0, one launch (start us, length us, event | category | flops | bytes accessed | tf_op | source)
XLA Modules:
  0.0 73.3 jit_solution(2153307610943517937)
XLA Ops:
  0.7 1.0 %rev.3 = bf16[16,8,3,49]{3,1,2,0:T(8,128)(2,1)S(1)} reverse(bf16[16,8,3,49]{3,1,2,0:T(8,128)(2,1)} %param.11), dimensions={2,3} | reverse | bytes 75264 | tf_op jit(solution)/shard_map/rev | solution.py:220
  1.7 0.0 copy-start.1
  1.7 0.0 copy-start.2
  1.7 1.0 %copy.16 = bf16[16,8,3,49]{3,2,1,0:T(4,128)(2,1)S(1)} copy(bf16[16,8,3,49]{3,1,2,0:T(8,128)(2,1)} %param.11) | data formatting | bytes 75264
  2.7 0.1 copy.17
  2.7 0.1 pad.16.clone
  2.8 0.2 reshape.166
  3.0 0.1 pad.14.clone
  3.1 0.2 reshape.165
  3.3 0.0 copy-done.1
  3.3 0.0 copy-done.2
  3.3 0.1 compare_and_fusion
  3.4 0.9 %select_convert_fusion = (f32[16,8,512]{2,1,0:T(8,128)}, f32[16,8,512]{2,1,0:T(8,128)}) fusion(bf16[16,8,432]{2,1,0:T(8,128)(2,1)S(1)} %reshape.166, pred[16,512]{1,0:T(8,128)(4,1)S(1)} %get-tuple-element.29, bf16[16,8,432]{2,1,0:T(8,128)(2,1)S(1)} %reshape.165, pred[16,512]{1,0:T(8,128)(4,1)S(1)} %get-tuple-element.30), kind=kLoop, calls=%fused_computation.1 | loop fusion | flops 262144 | bytes 761856 | tf_op jit(solution)/shard_map/convert_element_type | solution.py:221
  4.3 30.8 %shard_map.94 = (bf16[2048,256]{1,0:T(8,128)(2,1)}, bf16[96,256]{1,0:T(8,128)(2,1)}, bf16[96,256]{1,0:T(8,128)(2,1)}, bf16[18,24,256]{2,1,0:T(8,128)(2,1)}, bf16...) custom-call(f32[16,8,512]{2,1,0:T(8,128)} %get-tuple-element.32.base, ...), custom_call_target="tpu_custom_call" | custom-call | flops 4831838208 | bytes 4194304 | tf_op jit(solution)/shard_map/pallas_call | solution.py:236
  35.1 0.0 copy-start
  35.1 3.5 %all-to-all-start = ((bf16[32,64,256]{2,1,0:T(8,128)(2,1)}), bf16[32,64,256]{2,1,0:T(8,128)(2,1)S(1)}, u32[]{:S(2)}, u32[]{:S(2)}) async-start(bf16[32,64,256]{2,1,0:T(8,128)(2,1)} %bitcast.6), calls=%async_computation | async-start | bytes 2097152 | tf_op jit(solution)/shard_map/all_to_all | solution.py:261
  38.6 0.0 copy-done
  38.6 1.3 %copy.15 = bf16[8,256,256]{1,2,0:T(8,128)(2,1)} copy(bf16[8,256,256]{2,1,0:T(8,128)(2,1)S(1)} %bitcast.5) | data formatting | bytes 2097152 | tf_op jit(solution)/shard_map/reshape | solution.py:222
  40.0 32.5 %shard_map.95 = (bf16[16,96,256]{2,1,0:T(8,128)(2,1)}, bf16[16,96,256]{2,1,0:T(8,128)(2,1)}) custom-call(f32[16,8,512]{2,1,0:T(8,128)} %get-tuple-element.32.base, f32[16,8,512]{2,1,0:T(8,128)} %get-tuple-element.31.back, f32[8,512]{1,0:T(8,128)} %get-tuple-element.16.b_low, f32[8,512]{1,0:T(8,128)} %get-tuple-element.17.b_high, bf16[16,96,256]{2,1,0:T(8,128)(2,1)} %f_own.3, ...), custom_call_target="tpu_custom_call" | custom-call | flops 9663676416 | bytes 8388608 | tf_op jit(solution)/shard_map/pallas_call | solution.py:266
  72.5 0.0 all-to-all-done
  72.5 0.8 %convert_reduce_fusion = f32[64,256]{1,0:T(8,128)} fusion(bf16[32,64,256]{2,1,0:T(8,128)(2,1)S(1)} %all-to-all-done), kind=kLoop, calls=%fused_computation | loop fusion | flops 1032192 | bytes 1114112 | tf_op jit(solution)/shard_map/reduce_sum | solution.py:278
  (4 shorter events, 0.0 us)
Async XLA Ops:
  1.7 1.6 %copy-start.1 = (s32[16]{0:T(128)S(1)}, s32[16]{0:T(128)}, u32[]{:S(2)}) copy-start(s32[16]{0:T(128)} %param.12) | copy-start | bytes 196
  1.7 1.6 %copy-start.2 = (s32[16]{0:T(128)S(1)}, s32[16]{0:T(128)}, u32[]{:S(2)}) copy-start(s32[16]{0:T(128)} %param.13) | copy-start | bytes 196
  35.1 3.5 %copy-start = (bf16[2048,256]{1,0:T(8,128)(2,1)S(1)}, bf16[2048,256]{1,0:T(8,128)(2,1)}, u32[]{:S(2)}) copy-start(bf16[2048,256]{1,0:T(8,128)(2,1)} %weight.1) | copy-start | bytes 3145732
  35.1 37.4 %all-to-all-start = ((bf16[32,64,256]{2,1,0:T(8,128)(2,1)}), bf16[32,64,256]{2,1,0:T(8,128)(2,1)S(1)}, u32[]{:S(2)}, u32[]{:S(2)}) async-start(bf16[32,64,256]{2,1,0:T(8,128)(2,1)} %bitcast.6), calls=%async_computation | async-start | bytes 2097152 | tf_op jit(solution)/shard_map/all_to_all | solution.py:261

commit v2 on v1

--- a/solution.py
+++ b/solution.py
@@ -69,10 +69,10 @@
     count, lanes = taps.shape
     for k in range(count):
         start = jnp.broadcast_to(taps[k : k + 1, :], (16, lanes))
-        start = pltpu.roll(start, 0, 1, stride=1, stride_axis=0)
+        start = pltpu.roll(start, 0, 1, stride=1, stride_axis=0).astype(dest.dtype)
         for step in range(cols // 16):
             block = start if step == 0 else pltpu.roll(start, 16 * step, 1)
-            dest[k * cols + step * 16 : k * cols + (step + 1) * 16, :] = block.astype(dest.dtype)
+            dest[k * cols + step * 16 : k * cols + (step + 1) * 16, :] = block
 
 
 def convolve(toeplitz, field, row, span, conv, slot, cols, count):
@@ -81,7 +81,7 @@
     window = field[pl.ds(begin, toeplitz.shape[1]), :]
     result = jnp.dot(toeplitz[...], window, preferred_element_type=jnp.float32)
     result = result.astype(jnp.bfloat16)
-    place = pl.ds(pl.multiple_of(slot * cols, 16), cols)
+    place = slice(slot * cols, (slot + 1) * cols)
     for k in range(count):
         conv[place, k * chans : (k + 1) * chans] = result[k * cols : (k + 1) * cols, :]
 
@@ -117,25 +117,20 @@
                 device_id_type=MESH,
             )
         )
-    for copy in now + later:
+    for copy in now:
         copy.start()
-    build(base[0], even, cols)
     total[...] = jnp.zeros_like(total)
     for copy in now:
         copy.wait()
+    for copy in later:
+        copy.start()
     assemble(field, own, low, high, west, east, reach)
 
-    def pair(number, carry):
-        row = number * 2
-        slot = lax.rem(row, group)
-        build(base[row + 1], odd, cols)
-        convolve(even, field, row, span, conv, slot, cols, count)
-        build(base[lax.rem(row + 2, rows)], even, cols)
-        convolve(odd, field, row + 1, span, conv, slot + 1, cols, count)
-        return carry
-
     def several(step, carry):
-        lax.fori_loop(step * (group // 2), (step + 1) * (group // 2), pair, 0)
+        for slot in range(group):
+            toeplitz = (even, odd)[slot % 2]
+            build(base[step * group + slot], toeplitz, cols)
+            convolve(toeplitz, field, step * group + slot, span, conv, slot, cols, count)
         cotangent = g_own[pl.ds(step * group, group)].reshape(group * cols, chans)
         total[...] += lax.dot_general(
             cotangent, conv[...], (((0,), (0,)), ((), ())), preferred_element_type=jnp.float32
@@ -168,24 +163,14 @@
         taps[0] = b_low[...]
         taps[pl.ds(1, rows)] = back[...]
         taps[rows + 1] = b_high[...]
-        build(base[0], f_even, cols)
-        build(back_taps(0), g_even, cols)
-
-    def pair(number, carry):
-        slot = number * 2
+
+    for slot in range(group):
         row = step * group + slot
-        follow = lax.rem(row + 2, rows)
-        build(base[row + 1], f_odd, cols)
-        convolve(f_even, f_field, row, span, f_conv, slot, cols, count)
-        build(back_taps(row + 1), g_odd, cols)
-        convolve(g_even, g_field, row, span, g_conv, slot, cols, count)
-        build(base[follow], f_even, cols)
-        convolve(f_odd, f_field, row + 1, span, f_conv, slot + 1, cols, count)
-        build(back_taps(follow), g_even, cols)
-        convolve(g_odd, g_field, row + 1, span, g_conv, slot + 1, cols, count)
-        return carry
-
-    lax.fori_loop(0, group // 2, pair, 0)
+        f_square, g_square = ((f_even, g_even), (f_odd, g_odd))[slot % 2]
+        build(base[row], f_square, cols)
+        convolve(f_square, f_field, row, span, f_conv, slot, cols, count)
+        build(back_taps(row), g_square, cols)
+        convolve(g_square, g_field, row, span, g_conv, slot, cols, count)
     mixed = jnp.dot(f_conv[...], weight[...], preferred_element_type=jnp.float32)
     out[...] = mixed.astype(out.dtype).reshape(out.shape)
     mixed = jnp.dot(g_conv[...], weight_back[...], preferred_element_type=jnp.float32)

time: 73.6 us -> 62.7 us (0.85)
  Pallas kernels: 63.3 us -> 45.7 us
  waiting for transfers between devices: 0.01 us -> 7.54 us
    pallas_call x1, Pallas kernels: 32.5 us -> 17.3 us  [local(): pl.pallas_call(functools.partial(field_kernel, group, reach), grid=(steps...]
    all_to_all x1, waiting for transfers between devices: 0.01 us -> 7.54 us  [local(): lax.all_to_all(term.reshape(devices, weight.shape[0] // devices, chans),...]
    pallas_call x1, Pallas kernels: 30.8 us -> 28.4 us  [local(): pl.pallas_call(functools.partial(weight_kernel, group, reach), in_specs=[...]
  transfers between devices with their start and end apart: 1 -> 1, of which waited for: 0 -> 1; matrix products, arithmetic and copies ran while one was open for 2% -> 2% of each run, Pallas kernels for 44% -> 28%
where the time goes in v2:
time: 62.7 us; the launch traced here: 62.5 us
  Pallas kernels  45.7 us (73%)
  waiting for transfers between devices  7.54 us (12%)
  local copies, waits for them, and re-layouts  3.88 us (6%)
  starting transfers between devices  2.79 us (4%)
  other arithmetic  1.8 us (3%)
  between operations  0.78 us (1%)
    pallas_call x1, Pallas kernels, local(): pl.pallas_call(functools.partial(weight_kernel, group, reach), in_specs=[...  28.4 us
    pallas_call x1, Pallas kernels, local(): pl.pallas_call(functools.partial(field_kernel, group, reach), grid=(steps...  17.3 us
    all_to_all x1, waiting for transfers between devices, local(): lax.all_to_all(term.reshape(devices, weight.shape[0] // devices, chans),...  7.54 us
    all_to_all x1, starting transfers between devices, local(): lax.all_to_all(term.reshape(devices, weight.shape[0] // devices, chans),...  2.79 us
    reshape x1, local copies, waits for them, and re-layouts, local(): weight.reshape(count, chans, chans).transpose(0, 2, 1).reshape(weight.shape)  1.34 us
  transfers between devices with their start and end apart: 1, of which 1 were waited for; matrix products, arithmetic and copies ran while one was open for 2% of the time, Pallas kernels for 28%

profile of v2, /device:TPU:0, one launch (start us, length us, event | category | flops | bytes accessed | tf_op | source)
XLA Modules:
  0.0 62.5 jit_solution(17449577594033952783)
XLA Ops:
  0.7 1.0 %rev.3 = bf16[16,8,3,49]{3,1,2,0:T(8,128)(2,1)S(1)} reverse(bf16[16,8,3,49]{3,1,2,0:T(8,128)(2,1)} %param.11), dimensions={2,3} | reverse | bytes 75264 | tf_op jit(solution)/shard_map/rev | solution.py:205
  1.7 0.0 copy-start.1
  1.7 0.0 copy-start.2
  1.7 1.0 %copy.16 = bf16[16,8,3,49]{3,2,1,0:T(4,128)(2,1)S(1)} copy(bf16[16,8,3,49]{3,1,2,0:T(8,128)(2,1)} %param.11) | data formatting | bytes 75264
  2.7 0.1 copy.17
  2.7 0.1 pad.16.clone
  2.8 0.2 reshape.166
  3.0 0.1 pad.14.clone
  3.1 0.2 reshape.165
  3.3 0.0 copy-done.1
  3.3 0.0 copy-done.2
  3.3 0.1 compare_and_fusion
  3.4 0.9 %select_convert_fusion = (f32[16,8,512]{2,1,0:T(8,128)}, f32[16,8,512]{2,1,0:T(8,128)}) fusion(bf16[16,8,432]{2,1,0:T(8,128)(2,1)S(1)} %reshape.166, pred[16,512]{1,0:T(8,128)(4,1)S(1)} %get-tuple-element.29, bf16[16,8,432]{2,1,0:T(8,128)(2,1)S(1)} %reshape.165, pred[16,512]{1,0:T(8,128)(4,1)S(1)} %get-tuple-element.30), kind=kLoop, calls=%fused_computation.1 | loop fusion | flops 262144 | bytes 761856 | tf_op jit(solution)/shard_map/convert_element_type | solution.py:206
  4.3 28.4 %shard_map.94 = (bf16[2048,256]{1,0:T(8,128)(2,1)}, bf16[96,256]{1,0:T(8,128)(2,1)}, bf16[96,256]{1,0:T(8,128)(2,1)}, bf16[18,24,256]{2,1,0:T(8,128)(2,1)}, bf16...) custom-call(f32[16,8,512]{2,1,0:T(8,128)} %get-tuple-element.32.base, ...), custom_call_target="tpu_custom_call" | custom-call | flops 4831838208 | bytes 4194304 | tf_op jit(solution)/shard_map/pallas_call | solution.py:221
  32.7 0.0 copy-start
  32.7 2.8 %all-to-all-start = ((bf16[32,64,256]{2,1,0:T(8,128)(2,1)}), bf16[32,64,256]{2,1,0:T(8,128)(2,1)S(1)}, u32[]{:S(2)}, u32[]{:S(2)}) async-start(bf16[32,64,256]{2,1,0:T(8,128)(2,1)} %bitcast.6), calls=%async_computation | async-start | bytes 2097152 | tf_op jit(solution)/shard_map/all_to_all | solution.py:246
  35.5 0.0 copy-done
  35.5 1.3 %copy.15 = bf16[8,256,256]{1,2,0:T(8,128)(2,1)} copy(bf16[8,256,256]{2,1,0:T(8,128)(2,1)S(1)} %bitcast.5) | data formatting | bytes 2097152 | tf_op jit(solution)/shard_map/reshape | solution.py:207
  36.9 17.3 %shard_map.95 = (bf16[16,96,256]{2,1,0:T(8,128)(2,1)}, bf16[16,96,256]{2,1,0:T(8,128)(2,1)}) custom-call(f32[16,8,512]{2,1,0:T(8,128)} %get-tuple-element.32.base, f32[16,8,512]{2,1,0:T(8,128)} %get-tuple-element.31.back, f32[8,512]{1,0:T(8,128)} %get-tuple-element.16.b_low, f32[8,512]{1,0:T(8,128)} %get-tuple-element.17.b_high, bf16[16,96,256]{2,1,0:T(8,128)(2,1)} %f_own.3, ...), custom_call_target="tpu_custom_call" | custom-call | flops 9663676416 | bytes 8388608 | tf_op jit(solution)/shard_map/pallas_call | solution.py:251
  54.2 7.5 %all-to-all-done = bf16[32,64,256]{2,1,0:T(8,128)(2,1)S(1)} async-done(((bf16[32,64,256]{2,1,0:T(8,128)(2,1)}), bf16[32,64,256]{2,1,0:T(8,128)(2,1)S(1)}, u32[]{:S(2)}, u32[]{:S(2)}) %all-to-all-start) | async-done | bytes 1048608 | tf_op jit(solution)/shard_map/all_to_all | solution.py:246
  61.7 0.8 %convert_reduce_fusion = f32[64,256]{1,0:T(8,128)} fusion(bf16[32,64,256]{2,1,0:T(8,128)(2,1)S(1)} %all-to-all-done), kind=kLoop, calls=%fused_computation | loop fusion | flops 1032192 | bytes 1114112 | tf_op jit(solution)/shard_map/reduce_sum | solution.py:263
  (4 shorter events, 0.0 us)
Async XLA Ops:
  1.7 1.6 %copy-start.1 = (s32[16]{0:T(128)S(1)}, s32[16]{0:T(128)}, u32[]{:S(2)}) copy-start(s32[16]{0:T(128)} %param.12) | copy-start | bytes 196
  1.7 1.6 %copy-start.2 = (s32[16]{0:T(128)S(1)}, s32[16]{0:T(128)}, u32[]{:S(2)}) copy-start(s32[16]{0:T(128)} %param.13) | copy-start | bytes 196
  32.7 2.8 %copy-start = (bf16[2048,256]{1,0:T(8,128)(2,1)S(1)}, bf16[2048,256]{1,0:T(8,128)(2,1)}, u32[]{:S(2)}) copy-start(bf16[2048,256]{1,0:T(8,128)(2,1)} %weight.1) | copy-start | bytes 3145732
  32.7 29.0 %all-to-all-start = ((bf16[32,64,256]{2,1,0:T(8,128)(2,1)}), bf16[32,64,256]{2,1,0:T(8,128)(2,1)S(1)}, u32[]{:S(2)}, u32[]{:S(2)}) async-start(bf16[32,64,256]{2,1,0:T(8,128)(2,1)} %bitcast.6), calls=%async_computation | async-start | bytes 2097152 | tf_op jit(solution)/shard_map/all_to_all | solution.py:246
